TPU v7x, 32 devices: a whole 2x2x4 slice. The times are simulated.
32 devices in a mesh: depth: 4 (over z), row: 2 (over x), col: 4 (over y, core).
Axes of the slice: x: 2, y: 2, z: 4, core: 2. Of those that a mesh axis runs over, the one named last changes fastest.
Arguments:
- tokens: bfloat16 [192, 8192], P('row', ('depth', 'col')), may hold values from -6 to 6
- cotangent: bfloat16 [192, 8192], P('row', ('depth', 'col')), may hold values from -1.609375 to 1.609375
- gate_weight: bfloat16 [8192, 14336], P(('depth', 'col'), 'row'), may hold values from -0.0625 to 0.0625
- up_weight: bfloat16 [8192, 14336], P(('depth', 'col'), 'row'), may hold values from -0.0625 to 0.0625
- down_weight: bfloat16 [14336, 8192], P('row', ('depth', 'col')), may hold values from -0.046875 to 0.046875
Outputs:
- input_grad: bfloat16 [192, 8192], P('row', ('depth', 'col'))
- gate_grad: bfloat16 [8192, 14336], P(('depth', 'col'), 'row')
- up_grad: bfloat16 [8192, 14336], P(('depth', 'col'), 'row')
- down_grad: bfloat16 [14336, 8192], P('row', ('depth', 'col'))
All inputs are finite; a program needn't handle non-finite values.
Results may differ from a plain program's by a relative error of at most 0.0065.
Values may be sent and summed in bfloat16 or wider, within the bound.
No kernel may reach another device: no remote copies, remote signals or barrier semaphores. Data moves between devices by JAX's collectives and lax.ppermute only.
A program may use at most 128 MiB of HBM per device.

v0:
```python
import jax
import jax.numpy as jnp
from jax import lax
from jax.sharding import PartitionSpec as P


def swiglu_back(gate, up, back):
    sig = jax.nn.sigmoid(gate)
    hidden = (gate * sig * up).astype(jnp.bfloat16)
    grad_gate = (back * up * sig * (1.0 + gate * (1.0 - sig))).astype(jnp.bfloat16)
    grad_up = (back * gate * sig).astype(jnp.bfloat16)
    return (hidden, grad_gate, grad_up)


def contract_rows(left, right):
    return lax.dot_general(
        left, right, (((0,), (0,)), ((), ())), preferred_element_type=jnp.float32
    )


def contract_cols(left, right):
    return lax.dot_general(
        left, right, (((1,), (1,)), ((), ())), preferred_element_type=jnp.float32
    )


def stationary(tokens, cotangent, gate_weight, up_weight, down_weight):
    rows_all, cot_all = (
        lax.all_gather(tokens, "row", axis=0, tiled=True),
        lax.all_gather(cotangent, "row", axis=0, tiled=True),
    )
    width = gate_weight.shape[1]
    rows_part = rows_all
    cot_part = cot_all
    gate_part = jnp.dot(rows_part, gate_weight, preferred_element_type=jnp.float32)
    up_part = jnp.dot(rows_part, up_weight, preferred_element_type=jnp.float32)
    back_part = contract_cols(cot_part, down_weight)
    summed = lax.psum_scatter(
        jnp.concatenate([gate_part, up_part, back_part], axis=1),
        ("depth", "col"),
        scatter_dimension=0,
        tiled=True,
    )
    hidden, grad_gate, grad_up = swiglu_back(
        summed[:, :width], summed[:, width : 2 * width], summed[:, 2 * width :]
    )
    hidden_piece = lax.all_gather(hidden, ("depth", "col"), axis=0, tiled=True)
    gate_piece = lax.all_gather(grad_gate, ("depth", "col"), axis=0, tiled=True)
    up_piece = lax.all_gather(grad_up, ("depth", "col"), axis=0, tiled=True)
    rows_part = rows_all
    cot_part = cot_all
    acc_gate = contract_rows(rows_part, gate_piece)
    acc_up = contract_rows(rows_part, up_piece)
    acc_down = contract_rows(hidden_piece, cot_part)
    block = contract_cols(gate_piece, gate_weight) + contract_cols(up_piece, up_weight)
    input_grad = lax.psum_scatter(block, "row", scatter_dimension=0, tiled=True).astype(
        jnp.bfloat16
    )
    return (
        input_grad,
        acc_gate.astype(jnp.bfloat16),
        acc_up.astype(jnp.bfloat16),
        acc_down.astype(jnp.bfloat16),
    )


def on_device(tokens, cotangent, gate_weight, up_weight, down_weight):
    return stationary(tokens, cotangent, gate_weight, up_weight, down_weight)


def solution(mesh):
    return jax.shard_map(
        on_device,
        mesh=mesh,
        in_specs=(
            P("row", ("depth", "col")),
            P("row", ("depth", "col")),
            P(("depth", "col"), "row"),
            P(("depth", "col"), "row"),
            P("row", ("depth", "col")),
        ),
        out_specs=(
            P("row", ("depth", "col")),
            P(("depth", "col"), "row"),
            P(("depth", "col"), "row"),
            P("row", ("depth", "col")),
        ),
        check_vma=False,
    )
```

profile of v0, /device:TPU:0, one launch (start us, length us, event | category | flops | bytes accessed | tf_op | source)
XLA Modules:
  0.0 501.4 jit_solution(8831859143707906585)
XLA Ops:
  7.2 6.8 %all_gather.15 = bf16[192,512]{1,0:T(8,128)(2,1)S(1)} all-gather(bf16[96,512]{1,0:T(8,128)(2,1)} %param.5), channel_id=1, replica_groups=mesh['depth'=4,'row'=2,'col'=4] {'row'}, dimensions={0}, use_global_device_ids=true | all-gather | bytes 294912 | tf_op jit(solution)/shard_map/all_gather | solution.py:29
  14.0 4.8 fusion.5
  18.9 1.6 fusion.6
  20.5 5.3 %all_gather.16 = bf16[192,512]{1,0:T(8,128)(2,1)S(1)} all-gather(bf16[96,512]{1,0:T(8,128)(2,1)S(1)} %copy-done.1), channel_id=1, replica_groups=mesh['depth'=4,'row'=2,'col'=4] {'row'}, dimensions={0}, use_global_device_ids=true | all-gather | bytes 294912 | tf_op jit(solution)/shard_map/all_gather | solution.py:30
  25.8 5.6 %fusion.7 = f32[192,7168]{1,0:T(8,128)S(1)} fusion(bf16[192,512]{1,0:T(8,128)(2,1)S(1)} %all_gather.16, bf16[7168,512]{1,0:T(8,128)(2,1)} %param.9), kind=kOutput, calls=%fused_computation.16 | convolution fusion | flops 1409286144 | bytes 13041664 | tf_op jit(solution)/shard_map/dot_general | solution.py:22
  31.4 6.0 %pad_maximum_fusion = f32[192,21504]{1,0:T(8,128)} fusion(f32[192,7168]{1,0:T(8,128)S(1)} %fusion.7, f32[192,7168]{1,0:T(8,128)S(1)} %fusion.6, f32[192,7168]{1,0:T(8,128)S(1)} %fusion.5), kind=kLoop, calls=%fused_computation | loop fusion | flops 8257536 | bytes 33030144 | tf_op jit(solution)/shard_map/concatenate | solution.py:39
  39.2 292.3 %all-reduce.3.cloned.1.call-done = f32[192,21504]{1,0:T(8,128)} async-done(((f32[192,21504]{1,0:T(8,128)}), f32[192,21504]{1,0:T(8,128)}) %all-reduce.3.cloned.1.call-update) | async-done | bytes 16515088
  331.5 2.7 fusion.3
  334.3 0.7 all-gather.9.cloned.1.call-update
  335.8 46.3 %all-gather.7.cloned.1.call-done = bf16[16,12,7168]{2,1,0:T(8,128)(2,1)} async-done(((bf16[1,12,7168]{2,1,0:T(8,128)(2,1)}), bf16[16,12,7168]{2,1,0:T(8,128)(2,1)}) %all-gather.7.cloned.1.call-update) | async-done | bytes 2752528 | tf_op jit(solution)/shard_map/all_gather | solution.py:48
  382.1 3.0 reshape.9
  385.2 5.2 %fusion = bf16[512,7168]{0,1:T(8,128)(2,1)} fusion(bf16[192,7168]{1,0:T(8,128)(2,1)S(1)} %reshape.9, bf16[192,512]{1,0:T(8,128)(2,1)S(1)} %all_gather.15), kind=kOutput, calls=%fused_computation.4 | convolution fusion | flops 1412956160 | bytes 10289152 | tf_op jit(solution)/shard_map/dot_general | solution.py:16
  390.3 10.0 %copy.13 = bf16[512,7168]{1,0:T(8,128)(2,1)} copy(bf16[512,7168]{0,1:T(8,128)(2,1)} %fusion) | data formatting | bytes 14680064
  400.3 30.5 %all-gather.9.cloned.1.call-done = bf16[16,12,7168]{2,1,0:T(8,128)(2,1)} async-done(((bf16[1,12,7168]{2,1,0:T(8,128)(2,1)}), bf16[16,12,7168]{2,1,0:T(8,128)(2,1)}) %all-gather.9.cloned.1.call-update) | async-done | bytes 2752528 | tf_op jit(solution)/shard_map/all_gather | solution.py:49
  430.8 3.0 reshape.11
  433.8 6.5 %fusion.8 = f32[192,512]{1,0:T(8,128)S(1)} fusion(bf16[192,7168]{1,0:T(8,128)(2,1)} %copy-done, bf16[512,7168]{1,0:T(8,128)(2,1)} %param.7), kind=kOutput, calls=%fused_computation.17 | convolution fusion | flops 1409286144 | bytes 10485760 | tf_op jit(solution)/shard_map/dot_general | solution.py:22
  440.3 6.4 %convolution_add_fusion = f32[192,512]{1,0:T(8,128)} fusion(f32[192,512]{1,0:T(8,128)S(1)} %fusion.8, bf16[192,7168]{1,0:T(8,128)(2,1)S(1)} %reshape.11, bf16[512,7168]{1,0:T(8,128)(2,1)} %param.8), kind=kOutput, calls=%fused_computation.6 | convolution fusion | flops 1409384448 | bytes 10878976 | tf_op jit(solution)/shard_map/dot_general | solution.py:22
  446.7 5.2 %fusion.1 = bf16[512,7168]{0,1:T(8,128)(2,1)} fusion(bf16[192,7168]{1,0:T(8,128)(2,1)S(1)} %reshape.11, bf16[192,512]{1,0:T(8,128)(2,1)S(1)} %all_gather.15), kind=kOutput, calls=%fused_computation.5 | convolution fusion | flops 1412956160 | bytes 10289152 | tf_op jit(solution)/shard_map/dot_general | solution.py:16
  451.9 10.0 %copy.14 = bf16[512,7168]{1,0:T(8,128)(2,1)} copy(bf16[512,7168]{0,1:T(8,128)(2,1)} %fusion.1) | data formatting | bytes 14680064
  461.9 17.4 %all-gather.11.cloned.1.call-done = bf16[16,12,7168]{2,1,0:T(8,128)(2,1)} async-done(((bf16[1,12,7168]{2,1,0:T(8,128)(2,1)}), bf16[16,12,7168]{2,1,0:T(8,128)(2,1)}) %all-gather.11.cloned.1.call-update) | async-done | bytes 2752528 | tf_op jit(solution)/shard_map/all_gather | solution.py:47
  479.3 3.0 reshape.13
  482.4 5.2 %convolution_convert_fusion = bf16[7168,512]{1,0:T(8,128)(2,1)} fusion(bf16[192,7168]{1,0:T(8,128)(2,1)S(1)} %reshape.13, bf16[192,512]{1,0:T(8,128)(2,1)S(1)} %all_gather.16), kind=kOutput, calls=%fused_computation.1 | convolution fusion | flops 1412956160 | bytes 10289152 | tf_op jit(solution)/shard_map/dot_general | solution.py:16
  487.5 5.8 %reduce-scatter.2.cloned.1.call-done = f32[96,512]{1,0:T(8,128)} async-done(((f32[192,512]{1,0:T(8,128)}), f32[96,512]{1,0:T(8,128)}) %reduce-scatter.2.cloned.1.call-update) | async-done | bytes 196624 | tf_op jit(solution)/shard_map/reduce_scatter | solution.py:56
  493.3 1.6 convert_element_type.29
  (21 shorter events, 2.1 us)
Async XLA Ops:
  7.2 11.7 %slice-start = ((s8[7340032]{0:T(1024)(128)(4,1)}), s8[3145728]{0:T(1024)(128)(4,1)S(1)}, s32[]{:S(2)}) async-start(s8[7340032]{0:T(1024)(128)(4,1)} %bitcast.27), calls=%async_computation.6 | async-start | bytes 6291456
  7.2 324.3 %all-reduce.3.cloned.1.call-start = ((), (), s32[]{:S(2)}) async-start(), calls=%async_computation.5 | async-start | bytes 33030144
  14.0 4.9 slice-start.1
  18.9 1.6 copy-start.1
  37.4 0.7 copy-start.2
  37.4 344.7 %all-gather.7.cloned.1.call-start = ((), (), s32[]{:S(2)}) async-start(), calls=%async_computation.2 | async-start | bytes 3899392 | tf_op jit(solution)/shard_map/all_gather | solution.py:48
  334.3 96.5 %all-gather.9.cloned.1.call-start = ((), (), s32[]{:S(2)}) async-start(), calls=%async_computation.3 | async-start | bytes 3899392 | tf_op jit(solution)/shard_map/all_gather | solution.py:49
  335.0 144.3 %all-gather.11.cloned.1.call-start = ((), (), s32[]{:S(2)}) async-start(), calls=%async_computation.4 | async-start | bytes 3899392 | tf_op jit(solution)/shard_map/all_gather | solution.py:47
  335.6 157.8 %reduce-scatter.2.cloned.1.call-start = ((), (), s32[]{:S(2)}) async-start(), calls=%async_computation.1 | async-start | bytes 589824 | tf_op jit(solution)/shard_map/reduce_scatter | solution.py:56
  385.2 15.2 %copy-start = (bf16[192,7168]{1,0:T(8,128)(2,1)}, bf16[192,7168]{1,0:T(8,128)(2,1)S(1)}, u32[]{:S(2)}) copy-start(bf16[192,7168]{1,0:T(8,128)(2,1)S(1)} %reshape.9) | copy-start | bytes 8257540
Sparse Core Ops, SparseCore 0:
  37.5 293.9 all-reduce.2
  334.4 47.7 all-gather.6
  384.4 46.3 all-gather.8
  432.9 46.3 all-gather.10
  481.4 11.8 reduce-scatter.1
where the time goes:
time: 502 us; the launch traced here: 501 us
  waiting for transfers between devices  393 us (78%)
  matrix products  40.4 us (8%)
  local copies, waits for them, and re-layouts  30.3 us (6%)
  between operations  14.5 us (3%)
  blocking collectives  12.1 us (2%)
  other arithmetic  10.3 us (2%)
    unnamed x6, waiting for transfers between devices  294 us
    all_gather x1, waiting for transfers between devices, stationary(): gate_piece = lax.all_gather(grad_gate, ('depth', 'col'), axis=0, tiled=True)  46.3 us
    all_gather x1, waiting for transfers between devices, stationary(): up_piece = lax.all_gather(grad_up, ('depth', 'col'), axis=0, tiled=True)  30.5 us
    unnamed x16, local copies, waits for them, and re-layouts  30.3 us
    dot_general x3, matrix products, contract_cols(): lax.dot_general(left, right, (((1,), (1,)), ((), ())), preferred_element_...  18.5 us
    all_gather x1, waiting for transfers between devices, stationary(): hidden_piece = lax.all_gather(hidden, ('depth', 'col'), axis=0, tiled=True)  17.4 us
    dot_general x3, matrix products, contract_rows(): lax.dot_general(left, right, (((0,), (0,)), ((), ())), preferred_element_...  15.5 us
  transfers between devices with their start and end apart: 5, of which 5 were waited for; matrix products, arithmetic and copies ran while one was open for 12% of the time, Pallas kernels for 0%

commit v1 on v0

v1 whole, which is shorter than its diff:
```python
import jax
import jax.numpy as jnp
from jax import lax
from jax.experimental import pallas as pl
from jax.experimental.pallas import tpu as pltpu
from jax.sharding import PartitionSpec as P

LANES = 128
MIB = 1 << 20
F32 = jnp.float32
BF16 = jnp.bfloat16


def swiglu_back(gate, up, back):
    sig = jax.nn.sigmoid(gate)
    hidden = (gate * sig * up).astype(jnp.bfloat16)
    grad_gate = (back * up * sig * (1.0 + gate * (1.0 - sig))).astype(jnp.bfloat16)
    grad_up = (back * gate * sig).astype(jnp.bfloat16)
    return (hidden, grad_gate, grad_up)


def contract_rows(left, right):
    return lax.dot_general(
        left, right, (((0,), (0,)), ((), ())), preferred_element_type=jnp.float32
    )


def contract_cols(left, right):
    return lax.dot_general(
        left, right, (((1,), (1,)), ((), ())), preferred_element_type=jnp.float32
    )


def stationary(tokens, cotangent, gate_weight, up_weight, down_weight):
    rows_all, cot_all = (
        lax.all_gather(tokens, "row", axis=0, tiled=True),
        lax.all_gather(cotangent, "row", axis=0, tiled=True),
    )
    width = gate_weight.shape[1]
    gate_part = jnp.dot(rows_all, gate_weight, preferred_element_type=jnp.float32)
    up_part = jnp.dot(rows_all, up_weight, preferred_element_type=jnp.float32)
    back_part = contract_cols(cot_all, down_weight)
    summed = lax.psum_scatter(
        jnp.concatenate([gate_part, up_part, back_part], axis=1),
        ("depth", "col"),
        scatter_dimension=0,
        tiled=True,
    )
    hidden, grad_gate, grad_up = swiglu_back(
        summed[:, :width], summed[:, width : 2 * width], summed[:, 2 * width :]
    )
    hidden_piece = lax.all_gather(hidden, ("depth", "col"), axis=0, tiled=True)
    gate_piece = lax.all_gather(grad_gate, ("depth", "col"), axis=0, tiled=True)
    up_piece = lax.all_gather(grad_up, ("depth", "col"), axis=0, tiled=True)
    acc_gate = contract_rows(rows_all, gate_piece)
    acc_up = contract_rows(rows_all, up_piece)
    acc_down = contract_rows(hidden_piece, cot_all)
    block = contract_cols(gate_piece, gate_weight) + contract_cols(up_piece, up_weight)
    input_grad = lax.psum_scatter(block, "row", scatter_dimension=0, tiled=True)
    return tuple(a.astype(BF16) for a in (input_grad, acc_gate, acc_up, acc_down))


def swap(value, axis, mask, size):
    return lax.ppermute(value, axis, [(i, i ^ mask) for i in range(size)])


VMEM = pl.BlockSpec(memory_space=pltpu.VMEM)


def near(*arrays):
    return tuple(pltpu.with_memory_space_constraint(a, pltpu.VMEM) for a in arrays)


def estimate(flops, moved):
    return pl.CostEstimate(flops=flops, bytes_accessed=moved, transcendentals=0)


def order_kernel(where_ref, t_ref, c_ref, tp_ref, cp_ref, tt_ref):
    rows = t_ref.shape[0] // 4
    for q in range(4):
        start = pl.multiple_of((where_ref[1] ^ q) * rows, 16)
        tp_ref[q * rows : (q + 1) * rows, :] = t_ref[pl.ds(start, rows), :]
        cp_ref[q * rows : (q + 1) * rows, :] = c_ref[pl.ds(start, rows), :]
    tt_ref[...] = tp_ref[...].T


def order_rows(where, tokens, cot):
    n, d = tokens.shape
    return pl.pallas_call(
        order_kernel,
        in_specs=[pl.BlockSpec(memory_space=pltpu.SMEM), VMEM, VMEM],
        out_specs=[VMEM] * 3,
        out_shape=[
            pltpu.VMEM((n, d), BF16),
            pltpu.VMEM((n, d), BF16),
            pltpu.VMEM((d, n), BF16),
        ],
        cost_estimate=estimate(1 << 20, 5 * n * d * 2),
        compiler_params=pltpu.CompilerParams(vmem_limit_bytes=4 * MIB),
        name="order_rows",
    )(where, *near(tokens, cot))


def project_kernel(where_ref, t_ref, c_ref, wg_ref, wu_ref, wd_ref, keep_ref, send_ref):
    rows = t_ref.shape[0] // 4
    k = pl.program_id(0)
    tokens = t_ref[...]
    products = (
        lambda: jnp.dot(tokens, wg_ref[...], preferred_element_type=F32),
        lambda: jnp.dot(tokens, wu_ref[...], preferred_element_type=F32),
        lambda: contract_cols(c_ref[...], wd_ref[...]),
    )
    for i, product in enumerate(products):
        value = product()
        for y in range(2):
            keep_ref[k, y, i] = value[2 * y * rows : (2 * y + 1) * rows]
            send_ref[k, y, i] = value[(2 * y + 1) * rows : (2 * y + 2) * rows].astype(BF16)


def project(where, tokens, cot, gate_weight, up_weight, down_weight, base, width):
    n, d = tokens.shape
    rows = n // 4
    first = base // width
    columns = pl.BlockSpec((d, width), lambda k, s: (0, first + (s[0] ^ k)))
    down = pl.BlockSpec((width, d), lambda k, s: (first + (s[0] ^ k), 0))
    shape = (4, 2, 3, rows, width)
    return pl.pallas_call(
        project_kernel,
        grid_spec=pltpu.PrefetchScalarGridSpec(
            num_scalar_prefetch=1,
            grid=(4,),
            in_specs=[VMEM, VMEM, columns, columns, down],
            out_specs=[VMEM, VMEM],
        ),
        out_shape=[pltpu.VMEM(shape, F32), pltpu.VMEM(shape, BF16)],
        cost_estimate=estimate(6 * n * d * 4 * width, 3 * d * 4 * width * 2),
        compiler_params=pltpu.CompilerParams(vmem_limit_bytes=12 * MIB),
        name="project",
    )(where, *near(tokens, cot), gate_weight, up_weight, down_weight)


def halve_kernel(kept_ref, got_ref, keep_ref, send_ref):
    major, _, minor = kept_ref.shape[:3]

    @pl.loop(0, major * minor)
    def _(i):
        a, b = i // minor, i % minor
        keep_ref[a, b] = kept_ref[a, 0, b] + got_ref[a, 0, b].astype(F32)
        send_ref[a, b] = (kept_ref[a, 1, b] + got_ref[a, 1, b].astype(F32)).astype(BF16)


def halve(kept, got, major):
    r, w = kept.shape[-2:]
    minor = kept.size // (2 * major * r * w)
    kept = kept.reshape(major, 2, minor, r, w)
    got = got.reshape(major, 2, minor, r, w)
    shape = (major, minor, r, w)
    return pl.pallas_call(
        halve_kernel,
        in_specs=[VMEM, VMEM],
        out_specs=[VMEM, VMEM],
        out_shape=[pltpu.VMEM(shape, F32), pltpu.VMEM(shape, BF16)],
        cost_estimate=estimate(kept.size, kept.size * 9),
        compiler_params=pltpu.CompilerParams(vmem_limit_bytes=4 * MIB),
        name="halve",
    )(*near(kept, got))


def gate_kernel(kept_ref, got_ref, out_ref):
    gate, up, back = (kept_ref[i] + got_ref[i].astype(F32) for i in range(3))
    for i, value in enumerate(swiglu_back(gate, up, back)):
        out_ref[i] = value


def gate_rule(kept, got):
    return pl.pallas_call(
        gate_kernel,
        in_specs=[VMEM, VMEM],
        out_specs=VMEM,
        out_shape=pltpu.VMEM(kept.shape, BF16),
        cost_estimate=estimate(kept.size * 10, kept.size * 8),
        compiler_params=pltpu.CompilerParams(vmem_limit_bytes=4 * MIB),
        name="gate_rule",
    )(*near(kept, got))


def stack_kernel(*refs):
    for i, ref in enumerate(refs[:-1]):
        refs[-1][i] = ref[...]


def stack_blocks(*blocks):
    shape = (len(blocks), *blocks[0].shape)
    return pl.pallas_call(
        stack_kernel,
        in_specs=[VMEM] * len(blocks),
        out_specs=VMEM,
        out_shape=pltpu.VMEM(shape, BF16),
        cost_estimate=estimate(1 << 16, 16 * blocks[0].size),
        compiler_params=pltpu.CompilerParams(vmem_limit_bytes=4 * MIB),
        name="stack_blocks",
    )(*near(*blocks))


def rows_of(refs, i):
    k = pl.program_id(0)
    return jnp.concatenate([ref[k, i] for ref in refs], axis=0)


def input_kernel(where_ref, *refs):
    shares, (wg_ref, wu_ref, before_ref), (total_ref,) = refs[:4], refs[4:7], refs[7:]

    @pl.when(pl.program_id(0) == 0)
    def _():
        total_ref[...] = before_ref[...]

    total_ref[...] += contract_cols(rows_of(shares, 1), wg_ref[...]) + contract_cols(
        rows_of(shares, 2), wu_ref[...]
    )


def input_part(where, shares, gate_weight, up_weight, before, base, width):
    n, d = before.shape
    first = base // width
    columns = pl.BlockSpec((d, width), lambda k, s: (0, first + (s[0] ^ k)))
    return pl.pallas_call(
        input_kernel,
        grid_spec=pltpu.PrefetchScalarGridSpec(
            num_scalar_prefetch=1,
            grid=(4,),
            in_specs=[VMEM] * 4 + [columns, columns, VMEM],
            out_specs=VMEM,
        ),
        out_shape=pltpu.VMEM((n, d), F32),
        cost_estimate=estimate(4 * n * d * 4 * width, 2 * d * 4 * width * 2),
        compiler_params=pltpu.CompilerParams(vmem_limit_bytes=12 * MIB),
        name="input_part",
    )(where, *near(*shares), gate_weight, up_weight, *near(before))


def weight_kernel(where_ref, *refs):
    shares, (tt_ref, c_ref) = refs[:4], refs[4:6]
    gate_ref, up_ref, down_ref = refs[-3:]
    tokens = tt_ref[...]
    gate_ref[...] = jnp.dot(tokens, rows_of(shares, 1), preferred_element_type=F32).astype(BF16)
    up_ref[...] = jnp.dot(tokens, rows_of(shares, 2), preferred_element_type=F32).astype(BF16)
    down_ref[...] = contract_rows(rows_of(shares, 0), c_ref[...]).astype(BF16)


def weight_part(where, shares, tokens_t, cot, grads, shapes, base, width):
    n, d = cot.shape
    first = base // width
    columns = pl.BlockSpec((d, width), lambda k, s: (0, first + (s[0] ^ k)))
    down = pl.BlockSpec((width, d), lambda k, s: (first + (s[0] ^ k), 0))
    in_specs = [VMEM] * 6
    aliases = {}
    if grads:
        in_specs += [pl.BlockSpec(memory_space=pl.ANY)] * 3
        aliases = {7: 0, 8: 1, 9: 2}
    return pl.pallas_call(
        weight_kernel,
        grid_spec=pltpu.PrefetchScalarGridSpec(
            num_scalar_prefetch=1,
            grid=(4,),
            in_specs=in_specs,
            out_specs=[columns, columns, down],
        ),
        out_shape=[jax.ShapeDtypeStruct(s, BF16) for s in shapes],
        input_output_aliases=aliases,
        cost_estimate=estimate(6 * n * d * 4 * width, 3 * d * 4 * width * 2),
        compiler_params=pltpu.CompilerParams(vmem_limit_bytes=14 * MIB),
        name="weight_part",
    )(where, *near(*shares, tokens_t, cot), *grads)


def split_kernel(where_ref, total_ref, keep_ref, send_ref):
    rows = total_ref.shape[0] // 4
    row, col = where_ref[2], where_ref[1]
    for i in range(2):
        mine = pl.multiple_of((col ^ (2 * row + i)) * rows, 16)
        other = pl.multiple_of((col ^ (2 * (1 - row) + i)) * rows, 16)
        keep_ref[i * rows : (i + 1) * rows, :] = total_ref[pl.ds(mine, rows), :]
        send_ref[i * rows : (i + 1) * rows, :] = total_ref[pl.ds(other, rows), :]


def split_rows(where, total):
    n, d = total.shape
    return pl.pallas_call(
        split_kernel,
        in_specs=[pl.BlockSpec(memory_space=pltpu.SMEM), VMEM],
        out_specs=[VMEM, VMEM],
        out_shape=[pltpu.VMEM((n // 2, d), F32)] * 2,
        cost_estimate=estimate(1 << 20, 4 * n * d * 2),
        compiler_params=pltpu.CompilerParams(vmem_limit_bytes=4 * MIB),
        name="split_rows",
    )(where, *near(total))


def widths_of(columns):
    units = columns // (4 * LANES)
    return [2 * LANES] * (units // 2) + [LANES] * (units % 2)


DUE = {
    "project": -2.5,
    "beside": -1.0,
    "across": 2.0,
    "near": 3.0,
    "far": 4.0,
    "forward": 5.0,
    "stack": 6.0,
    "corner": 8.0,
    "inputs": 8.5,
    "weights": 10.5,
}
LATER = 0.75


def order_of(count):
    due = [(at + LATER * i, i, stage) for i in range(count) for stage, at in DUE.items()]
    return [(stage, i) for _, i, stage in sorted(due, key=lambda entry: entry[:2])]


def halving(tokens, cotangent, gate_weight, up_weight, down_weight):
    return halving_steps(tokens, cotangent, gate_weight, up_weight, down_weight)


def halving_steps(tokens, cotangent, gate_weight, up_weight, down_weight):
    where = jnp.stack(
        [lax.axis_index("depth"), lax.axis_index("col"), lax.axis_index("row")]
    ).astype(jnp.int32)
    first_row = lax.axis_index("row") == 0

    def both(own):
        other = swap(own, "row", 1, 2)
        return jnp.where(
            first_row,
            jnp.concatenate([own, other], axis=0),
            jnp.concatenate([other, own], axis=0),
        )

    tokens_all, cot_all, tokens_t = order_rows(where, both(tokens), both(cotangent))
    n, d = tokens_all.shape
    rows = n // 4
    widths = widths_of(gate_weight.shape[1])
    bases = [4 * sum(widths[:i]) for i in range(len(widths))]
    shapes = (gate_weight.shape, up_weight.shape, down_weight.shape)
    state = {"total": jnp.zeros((n, d), F32), "grads": (), "last": tokens_t}

    def after(*arrays):
        *arrays, _ = lax.optimization_barrier((*arrays, state["last"]))
        return arrays

    def ran(value):
        state["last"] = value

    def piece(base, width):
        def shaped(value, *lead):
            return value.reshape(*lead, 3, rows, width)

        def send(value, axis, mask):
            return swap(value, axis, mask, 4)

        yield
        (t,) = after(tokens_all)
        kept, sent = project(where, t, cot_all, gate_weight, up_weight, down_weight, base, width)
        ran(sent)
        got = send(sent, "col", 1)
        yield
        kept, got = after(kept, got)
        kept, sent = halve(kept, got, 4)
        ran(sent)
        got = send(sent, "col", 2)
        yield
        kept, got = after(kept, got)
        kept, sent = halve(shaped(kept, 4), shaped(got, 4), 2)
        ran(sent)
        got = send(sent, "depth", 1)
        yield
        kept, got = after(kept, got)
        kept, sent = halve(shaped(kept, 2), shaped(got, 2), 1)
        ran(sent)
        got = send(sent, "depth", 2)
        yield
        kept, got = after(kept, got)
        mine = gate_rule(shaped(kept), shaped(got))
        ran(mine)
        second = send(mine, "depth", 2)
        first = send(mine, "depth", 1)
        yield
        (second,) = after(second)
        ran(second)
        third = send(second, "depth", 1)
        yield
        mine, first, second, third = after(mine, first, second, third)
        own = stack_blocks(mine, first, second, third)
        ran(own)
        across = send(own, "col", 2)
        beside = send(own, "col", 1)
        yield
        (across,) = after(across)
        ran(across)
        corner = send(across, "col", 1)
        yield
        own, beside, across, corner = after(own, beside, across, corner)
        shares = (own, beside, across, corner)
        state["total"] = input_part(where, shares, gate_weight, up_weight, state["total"], base, width)
        ran(state["total"])
        yield
        own, beside, across, corner = after(own, beside, across, corner)
        shares = (own, beside, across, corner)
        state["grads"] = weight_part(where, shares, tokens_t, cot_all, state["grads"], shapes, base, width)
        ran(state["grads"][0])

    pieces = [piece(base, width) for base, width in zip(bases, widths)]
    for running in pieces:
        next(running)
    for _, i in order_of(len(pieces)):
        next(pieces[i], None)

    keep, send = split_rows(where, state["total"])
    input_grad = (keep + swap(send, "row", 1, 2)).astype(BF16)
    return (input_grad, *state["grads"])


def fits(sizes, n_tokens, columns):
    mesh_fits = (sizes["depth"], sizes["row"], sizes["col"]) == (4, 2, 4)
    return mesh_fits and n_tokens % 64 == 0 and columns % (4 * LANES) == 0


def solution(mesh):
    sizes = dict(mesh.shape)

    def step(tokens, cotangent, gate_weight, up_weight, down_weight):
        args = (tokens, cotangent, gate_weight, up_weight, down_weight)
        columns = gate_weight.shape[1] // sizes["row"]
        halves = fits(sizes, tokens.shape[0], columns)
        mapped = jax.shard_map(
            halving if halves else stationary,
            mesh=mesh,
            in_specs=(
                P("row", ("depth", "col")),
                P("row", ("depth", "col")),
                P(("depth", "col"), "row"),
                P(("depth", "col"), "row"),
                P("row", ("depth", "col")),
            ),
            out_specs=(
                P("row", ("depth", "col")),
                P(("depth", "col"), "row"),
                P(("depth", "col"), "row"),
                P("row", ("depth", "col")),
            ),
            check_vma=False,
        )
        return mapped(*args)

    return step
```

time: 502 us -> 209 us (0.42)
  waiting for transfers between devices: 393 us -> 60.7 us
  starting transfers between devices: 0.38 us -> 74.3 us
  Pallas kernels: 0 us -> 60.4 us
  matrix products: 40.4 us -> 0 us
  local copies, waits for them, and re-layouts: 30.3 us -> 9.32 us
  between operations: 14.5 us -> 1.37 us
  blocking collectives: 12.1 us -> 0 us
  other arithmetic: 10.3 us -> 2.76 us
    unnamed x6 -> x0, waiting for transfers between devices: 294 us -> none
    all_gather x3 -> x0, waiting for transfers between devices: 94.2 us -> none  [the longest x1 46.3 us: stationary(): gate_piece = lax.all_gather(grad_gate, ('depth', 'col'), axis=0, tiled=True)]
    ppermute x0 -> x73, starting transfers between devices: none -> 74.3 us  [swap(): return lax.ppermute(value, axis, [(i, i ^ mask) for i in range(size)])]
    ppermute x0 -> x73, waiting for transfers between devices: none -> 60.7 us  [swap(): return lax.ppermute(value, axis, [(i, i ^ mask) for i in range(size)])]
    pallas_call x0 -> x58, Pallas kernels: none -> 60.4 us  [the longest x7 23.1 us: weight_part(): pl.pallas_call(weight_kernel, grid_spec=pltpu.PrefetchScalarGridSpec(num_...]
    dot_general x8 -> x0, matrix products: 40.4 us -> none  [the longest x3 18.5 us: contract_cols(): lax.dot_general(left, right, (((1,), (1,)), ((), ())), preferred_element_...]
    unnamed x16 -> x14, local copies, waits for them, and re-layouts: 30.3 us -> 9.29 us
    all_gather x2 -> x0, blocking collectives: 12.1 us -> none  [the longest x1 6.78 us: stationary(): lax.all_gather(tokens, 'row', axis=0, tiled=True)]
  transfers between devices with their start and end apart: 5 -> 73, of which waited for: 5 -> 28; matrix products, arithmetic and copies ran while one was open for 12% -> 1% of each run, Pallas kernels for 0% -> 26%
where the time goes in v1:
time: 209 us
  starting transfers between devices  74.3 us (36%)
  waiting for transfers between devices  60.7 us (29%)
  Pallas kernels  60.4 us (29%)
  local copies, waits for them, and re-layouts  9.32 us (4%)
  other arithmetic  2.76 us (1%)
    ppermute x73, starting transfers between devices, swap(): return lax.ppermute(value, axis, [(i, i ^ mask) for i in range(size)])  74.3 us
    ppermute x73, waiting for transfers between devices, swap(): return lax.ppermute(value, axis, [(i, i ^ mask) for i in range(size)])  60.7 us
    pallas_call x7, Pallas kernels, weight_part(): pl.pallas_call(weight_kernel, grid_spec=pltpu.PrefetchScalarGridSpec(num_...  23.1 us
    pallas_call x7, Pallas kernels, project(): pl.pallas_call(project_kernel, grid_spec=pltpu.PrefetchScalarGridSpec(num...  16.3 us
    pallas_call x7, Pallas kernels, input_part(): pl.pallas_call(input_kernel, grid_spec=pltpu.PrefetchScalarGridSpec(num_s...  16 us
    unnamed x14, local copies, waits for them, and re-layouts  9.29 us
  transfers between devices with their start and end apart: 73, of which 28 were waited for; matrix products, arithmetic and copies ran while one was open for 1% of the time, Pallas kernels for 26%

profile of v1, /device:TPU:0, one launch (start us, length us, event | category | flops | bytes accessed | tf_op | source)
XLA Modules:
  0.0 208.8 jit_solution(15216710907133084919)
XLA Ops:
  0.6 3.0 %collective-permute-start = (bf16[96,512]{1,0:T(8,128)(2,1)}, bf16[96,512]{1,0:T(8,128)(2,1)S(1)}, u32[]{:S(2)}, u32[]{:S(2)}) collective-permute-start(bf16[96,512]{1,0:T(8,128)(2,1)} %param.5), channel_id=1, source_target_pairs={{0,4},{4,0},{1,5},{5,1},{2,6},{6,2},{3,7},{7,3},{8,12},{12,8},{9,1... | collective-permute-start | bytes 294920 | tf_op jit(solution)/shard_map/ppermute | solution.py:64
  3.8 3.5 %collective-permute-done = bf16[96,512]{1,0:T(8,128)(2,1)S(1)} collective-permute-done((bf16[96,512]{1,0:T(8,128)(2,1)}, bf16[96,512]{1,0:T(8,128)(2,1)S(1)}, u32[]{:S(2)}, u32[]{:S(2)}) %collective-permute-start) | collective-permute-done | bytes 98336 | tf_op jit(solution)/shard_map/ppermute | solution.py:64
  10.5 3.1 %copy-done = bf16[512,7168]{1,0:T(8,128)(2,1)S(1)} copy-done((bf16[512,7168]{1,0:T(8,128)(2,1)S(1)}, bf16[512,7168]{1,0:T(8,128)(2,1)}, u32[]{:S(2)}) %copy-start) | copy-done | bytes 7340056
  13.6 3.1 %copy-done.1 = bf16[512,7168]{1,0:T(8,128)(2,1)S(1)} copy-done((bf16[512,7168]{1,0:T(8,128)(2,1)S(1)}, bf16[512,7168]{1,0:T(8,128)(2,1)}, u32[]{:S(2)}) %copy-start.1) | copy-done | bytes 7340056
  16.7 3.1 %copy-done.2 = bf16[7168,512]{1,0:T(8,128)(2,1)S(1)} copy-done((bf16[7168,512]{1,0:T(8,128)(2,1)S(1)}, bf16[7168,512]{1,0:T(8,128)(2,1)}, u32[]{:S(2)}) %copy-start.2) | copy-done | bytes 7340056
  38.4 4.8 %collective-permute-done.6 = bf16[4,3,48,256]{3,2,1,0:T(8,128)(2,1)S(1)} collective-permute-done((bf16[4,3,48,256]{3,2,1,0:T(8,128)(2,1)S(1)}, bf16[4,3,48,256]{3,2,1,0:T(8,128)(2,1)S(1)}, u32[]{:S(2)}, u32[]{:S(2)}) %collective-permute-start.6) | collective-permute-done | bytes 294944 | tf_op jit(solution)/shard_map/ppermute | solution.py:64
  49.9 6.1 %collective-permute-done.12 = bf16[4,3,48,256]{3,2,1,0:T(8,128)(2,1)S(1)} collective-permute-done((bf16[4,3,48,256]{3,2,1,0:T(8,128)(2,1)S(1)}, bf16[4,3,48,256]{3,2,1,0:T(8,128)(2,1)S(1)}, u32[]{:S(2)}, u32[]{:S(2)}) %collective-permute-start.12) | collective-permute-done | bytes 294944 | tf_op jit(solution)/shard_map/ppermute | solution.py:64
  64.3 2.6 %collective-permute-start.16 = (bf16[1,3,48,256]{3,2,1,0:T(8,128)(2,1)S(1)}, bf16[1,3,48,256]{3,2,1,0:T(8,128)(2,1)S(1)}, u32[]{:S(2)}, u32[]{:S(2)}) collective-permute-start(bf16[1,3,48,256]{3,2,1,0:T(8,128)(2,1)S(1)} %get-tuple-element.301), channel_id=1, source_target_pairs={{0,16},{8,24},{16,0},{24,8},{1,17},{9,25},{17,1},{25,9},{2,18},{10... | collective-permute-start | bytes 221192 | tf_op jit(solution)/shard_map/ppermute | solution.py:64
  79.9 4.3 %collective-permute-done.18 = bf16[1,3,48,256]{3,2,1,0:T(8,128)(2,1)S(1)} collective-permute-done((bf16[1,3,48,256]{3,2,1,0:T(8,128)(2,1)S(1)}, bf16[1,3,48,256]{3,2,1,0:T(8,128)(2,1)S(1)}, u32[]{:S(2)}, u32[]{:S(2)}) %collective-permute-start.18) | collective-permute-done | bytes 73760 | tf_op jit(solution)/shard_map/ppermute | solution.py:64
  88.1 2.6 %collective-permute-start.24 = (bf16[1,3,48,256]{3,2,1,0:T(8,128)(2,1)S(1)}, bf16[1,3,48,256]{3,2,1,0:T(8,128)(2,1)S(1)}, u32[]{:S(2)}, u32[]{:S(2)}) collective-permute-start(bf16[1,3,48,256]{3,2,1,0:T(8,128)(2,1)S(1)} %get-tuple-element.336), channel_id=1, source_target_pairs={{0,16},{8,24},{16,0},{24,8},{1,17},{9,25},{17,1},{25,9},{2,18},{10... | collective-permute-start | bytes 221192 | tf_op jit(solution)/shard_map/ppermute | solution.py:64
  99.4 2.8 %collective-permute-start.34 = (bf16[1,3,48,256]{3,2,1,0:T(8,128)(2,1)S(1)}, bf16[1,3,48,256]{3,2,1,0:T(8,128)(2,1)S(1)}, u32[]{:S(2)}, u32[]{:S(2)}) collective-permute-start(bf16[1,3,48,256]{3,2,1,0:T(8,128)(2,1)S(1)} %get-tuple-element.352), channel_id=1, source_target_pairs={{0,16},{8,24},{16,0},{24,8},{1,17},{9,25},{17,1},{25,9},{2,18},{10... | collective-permute-start | bytes 221192 | tf_op jit(solution)/shard_map/ppermute | solution.py:64
  114.7 4.3 %collective-permute-done.41 = bf16[1,3,48,256]{3,2,1,0:T(8,128)(2,1)S(1)} collective-permute-done((bf16[1,3,48,256]{3,2,1,0:T(8,128)(2,1)S(1)}, bf16[1,3,48,256]{3,2,1,0:T(8,128)(2,1)S(1)}, u32[]{:S(2)}, u32[]{:S(2)}) %collective-permute-start.41) | collective-permute-done | bytes 73760 | tf_op jit(solution)/shard_map/ppermute | solution.py:64
  120.1 2.9 %collective-permute-start.45 = (bf16[3,48,256]{2,1,0:T(8,128)(2,1)S(1)}, bf16[3,48,256]{2,1,0:T(8,128)(2,1)S(1)}, u32[]{:S(2)}, u32[]{:S(2)}) collective-permute-start(bf16[3,48,256]{2,1,0:T(8,128)(2,1)S(1)} %gate_rule.11.refs_0_), channel_id=1, source_target_pairs={{0,16},{8,24},{16,0},{24,8},{1,17},{9,25},{17,1},{25,9},{2,18},{10... | collective-permute-start | bytes 221192 | tf_op jit(solution)/shard_map/ppermute | solution.py:64
  137.4 3.3 %collective-permute-done.54.refs_2_ = bf16[3,48,256]{2,1,0:T(8,128)(2,1)S(1)} collective-permute-done((bf16[3,48,256]{2,1,0:T(8,128)(2,1)S(1)}, bf16[3,48,256]{2,1,0:T(8,128)(2,1)S(1)}, u32[]{:S(2)}, u32[]{:S(2)}) %collective-permute-start.54) | collective-permute-done | bytes 73760 | tf_op jit(solution)/shard_map/ppermute | solution.py:64
  141.4 3.7 %collective-permute-done.53.refs_3_ = bf16[3,48,256]{2,1,0:T(8,128)(2,1)S(1)} collective-permute-done((bf16[3,48,256]{2,1,0:T(8,128)(2,1)S(1)}, bf16[3,48,256]{2,1,0:T(8,128)(2,1)S(1)}, u32[]{:S(2)}, u32[]{:S(2)}) %collective-permute-start.53) | collective-permute-done | bytes 73760 | tf_op jit(solution)/shard_map/ppermute | solution.py:64
  151.3 3.7 %collective-permute-done.47.refs_2_ = bf16[3,48,256]{2,1,0:T(8,128)(2,1)S(1)} collective-permute-done((bf16[3,48,256]{2,1,0:T(8,128)(2,1)S(1)}, bf16[3,48,256]{2,1,0:T(8,128)(2,1)S(1)}, u32[]{:S(2)}, u32[]{:S(2)}) %collective-permute-start.47) | collective-permute-done | bytes 73760 | tf_op jit(solution)/shard_map/ppermute | solution.py:64
  155.3 4.1 %collective-permute-done.60.refs_3_ = bf16[3,48,256]{2,1,0:T(8,128)(2,1)S(1)} collective-permute-done((bf16[3,48,256]{2,1,0:T(8,128)(2,1)S(1)}, bf16[3,48,256]{2,1,0:T(8,128)(2,1)S(1)}, u32[]{:S(2)}, u32[]{:S(2)}) %collective-permute-start.60) | collective-permute-done | bytes 73760 | tf_op jit(solution)/shard_map/ppermute | solution.py:64
  165.3 3.3 %weight_part.7 = (bf16[512,7168]{1,0:T(8,128)(2,1)}, bf16[512,7168]{1,0:T(8,128)(2,1)}, bf16[7168,512]{1,0:T(8,128)(2,1)}) custom-call(s32[3]{0:T(128)S(1)} %pad_add_fusion.where_ref, bf16[4,3,48,256]{3,2,1,0:T(8,128)(2,1)S(1)} %stack_blocks.7.refs_0_, bf16[4,3,48,256]{3,2,1,0:T(8,128)(2,1)S(1)} %collective-permute-done.39.refs_1_, ...), custom_call_target="tpu_custom_call" | custom-call | flops 603979776 | bytes 3145728 | tf_op jit(solution)/shard_map/weight_part/pallas_call | solution.py:260
  172.8 3.3 %weight_part.8 = (bf16[512,7168]{1,0:T(8,128)(2,1)}, bf16[512,7168]{1,0:T(8,128)(2,1)}, bf16[7168,512]{1,0:T(8,128)(2,1)}) custom-call(s32[3]{0:T(128)S(1)} %pad_add_fusion.where_ref, bf16[4,3,48,256]{3,2,1,0:T(8,128)(2,1)S(1)} %stack_blocks.8.refs_0_, ...), custom_call_target="tpu_custom_call", output_to_operand_aliasing={{0}: (7, {}), {1}: (8, {}), {2}: (9, {})} | custom-call | flops 603979776 | bytes 3145728 | tf_op jit(solution)/shard_map/weight_part/pallas_call | solution.py:260
  182.3 3.3 %weight_part.9 = (bf16[512,7168]{1,0:T(8,128)(2,1)}, bf16[512,7168]{1,0:T(8,128)(2,1)}, bf16[7168,512]{1,0:T(8,128)(2,1)}) custom-call(s32[3]{0:T(128)S(1)} %pad_add_fusion.where_ref, bf16[4,3,48,256]{3,2,1,0:T(8,128)(2,1)S(1)} %stack_blocks.9.refs_0_, ...), custom_call_target="tpu_custom_call", output_to_operand_aliasing={{0}: (7, {}), {1}: (8, {}), {2}: (9, {})} | custom-call | flops 603979776 | bytes 3145728 | tf_op jit(solution)/shard_map/weight_part/pallas_call | solution.py:260
  190.4 3.3 %weight_part.10 = (bf16[512,7168]{1,0:T(8,128)(2,1)}, bf16[512,7168]{1,0:T(8,128)(2,1)}, bf16[7168,512]{1,0:T(8,128)(2,1)}) custom-call(s32[3]{0:T(128)S(1)} %pad_add_fusion.where_ref, bf16[4,3,48,256]{3,2,1,0:T(8,128)(2,1)S(1)} %stack_blocks.10.refs_0_, ...), custom_call_target="tpu_custom_call", output_to_operand_aliasing={{0}: (7, {}), {1}: (8, {}), {2}: (9, {})} | custom-call | flops 603979776 | bytes 3145728 | tf_op jit(solution)/shard_map/weight_part/pallas_call | solution.py:260
  198.2 3.3 %weight_part.11 = (bf16[512,7168]{1,0:T(8,128)(2,1)}, bf16[512,7168]{1,0:T(8,128)(2,1)}, bf16[7168,512]{1,0:T(8,128)(2,1)}) custom-call(s32[3]{0:T(128)S(1)} %pad_add_fusion.where_ref, bf16[4,3,48,256]{3,2,1,0:T(8,128)(2,1)S(1)} %stack_blocks.11.refs_0_, ...), custom_call_target="tpu_custom_call", output_to_operand_aliasing={{0}: (7, {}), {1}: (8, {}), {2}: (9, {})} | custom-call | flops 603979776 | bytes 3145728 | tf_op jit(solution)/shard_map/weight_part/pallas_call | solution.py:260
  201.5 3.3 %weight_part.12 = (bf16[512,7168]{1,0:T(8,128)(2,1)}, bf16[512,7168]{1,0:T(8,128)(2,1)}, bf16[7168,512]{1,0:T(8,128)(2,1)}) custom-call(s32[3]{0:T(128)S(1)} %pad_add_fusion.where_ref, bf16[4,3,48,256]{3,2,1,0:T(8,128)(2,1)S(1)} %stack_blocks.12.refs_0_, ...), custom_call_target="tpu_custom_call", output_to_operand_aliasing={{0}: (7, {}), {1}: (8, {}), {2}: (9, {})} | custom-call | flops 603979776 | bytes 3145728 | tf_op jit(solution)/shard_map/weight_part/pallas_call | solution.py:260
  204.8 3.3 %weight_part.13 = (bf16[512,7168]{1,0:T(8,128)(2,1)}, bf16[512,7168]{1,0:T(8,128)(2,1)}, bf16[7168,512]{1,0:T(8,128)(2,1)}) custom-call(s32[3]{0:T(128)S(1)} %pad_add_fusion.where_ref, bf16[4,3,48,256]{3,2,1,0:T(8,128)(2,1)S(1)} %stack_blocks.13.refs_0_, ...), custom_call_target="tpu_custom_call", output_to_operand_aliasing={{0}: (7, {}), {1}: (8, {}), {2}: (9, {})} | custom-call | flops 603979776 | bytes 3145728 | tf_op jit(solution)/shard_map/weight_part/pallas_call | solution.py:260
  (201 shorter events, 123.4 us)
Async XLA Ops:
  38.2 21.3 %collective-permute-start.11 = (bf16[4,2,3,48,256]{4,3,2,1,0:T(8,128)(2,1)S(1)}, bf16[4,2,3,48,256]{4,3,2,1,0:T(8,128)(2,1)S(1)}, u32[]{:S(2)}, u32[]{:S(2)}) collective-permute-start(bf16[4,2,3,48,256]{4,3,2,1,0:T(8,128)(2,1)S(1)} %get-tuple-element.279), channel_id=1, source_target_pairs={{0,1},{1,0},{2,3},{3,2},{4,5},{5,4},{6,7},{7,6},{8,9},{9,8},{10,11... | collective-permute-start | bytes 1769480 | tf_op jit(solution)/shard_map/ppermute | solution.py:64
  46.0 20.9 %collective-permute-start.8 = (bf16[4,2,3,48,256]{4,3,2,1,0:T(8,128)(2,1)S(1)}, bf16[4,2,3,48,256]{4,3,2,1,0:T(8,128)(2,1)S(1)}, u32[]{:S(2)}, u32[]{:S(2)}) collective-permute-start(bf16[4,2,3,48,256]{4,3,2,1,0:T(8,128)(2,1)S(1)} %get-tuple-element.288), channel_id=1, source_target_pairs={{0,1},{1,0},{2,3},{3,2},{4,5},{5,4},{6,7},{7,6},{8,9},{9,8},{10,11... | collective-permute-start | bytes 1769480 | tf_op jit(solution)/shard_map/ppermute | solution.py:64
  47.9 14.5 %collective-permute-start.9 = (bf16[4,3,48,256]{3,2,1,0:T(8,128)(2,1)S(1)}, bf16[4,3,48,256]{3,2,1,0:T(8,128)(2,1)S(1)}, u32[]{:S(2)}, u32[]{:S(2)}) collective-permute-start(bf16[4,3,48,256]{3,2,1,0:T(8,128)(2,1)S(1)} %get-tuple-element.269), channel_id=1, source_target_pairs={{0,2},{1,3},{2,0},{3,1},{4,6},{5,7},{6,4},{7,5},{8,10},{9,11},{10,... | collective-permute-start | bytes 884744 | tf_op jit(solution)/shard_map/ppermute | solution.py:64
  56.0 16.2 %collective-permute-start.15 = (bf16[4,3,48,256]{3,2,1,0:T(8,128)(2,1)S(1)}, bf16[4,3,48,256]{3,2,1,0:T(8,128)(2,1)S(1)}, u32[]{:S(2)}, u32[]{:S(2)}) collective-permute-start(bf16[4,3,48,256]{3,2,1,0:T(8,128)(2,1)S(1)} %get-tuple-element.277), channel_id=1, source_target_pairs={{0,2},{1,3},{2,0},{3,1},{4,6},{5,7},{6,4},{7,5},{8,10},{9,11},{10,... | collective-permute-start | bytes 884744 | tf_op jit(solution)/shard_map/ppermute | solution.py:64
  59.5 15.5 %collective-permute-start.20 = (bf16[4,3,48,256]{3,2,1,0:T(8,128)(2,1)S(1)}, bf16[4,3,48,256]{3,2,1,0:T(8,128)(2,1)S(1)}, u32[]{:S(2)}, u32[]{:S(2)}) collective-permute-start(bf16[4,3,48,256]{3,2,1,0:T(8,128)(2,1)S(1)} %get-tuple-element.285), channel_id=1, source_target_pairs={{0,2},{1,3},{2,0},{3,1},{4,6},{5,7},{6,4},{7,5},{8,10},{9,11},{10,... | collective-permute-start | bytes 884744 | tf_op jit(solution)/shard_map/ppermute | solution.py:64
  66.9 21.2 %collective-permute-start.28 = (bf16[4,3,48,256]{3,2,1,0:T(8,128)(2,1)S(1)}, bf16[4,3,48,256]{3,2,1,0:T(8,128)(2,1)S(1)}, u32[]{:S(2)}, u32[]{:S(2)}) collective-permute-start(bf16[4,3,48,256]{3,2,1,0:T(8,128)(2,1)S(1)} %get-tuple-element.298), channel_id=1, source_target_pairs={{0,2},{1,3},{2,0},{3,1},{4,6},{5,7},{6,4},{7,5},{8,10},{9,11},{10,... | collective-permute-start | bytes 884744 | tf_op jit(solution)/shard_map/ppermute | solution.py:64
  73.0 13.4 %collective-permute-start.19 = (bf16[2,3,48,256]{3,2,1,0:T(8,128)(2,1)S(1)}, bf16[2,3,48,256]{3,2,1,0:T(8,128)(2,1)S(1)}, u32[]{:S(2)}, u32[]{:S(2)}) collective-permute-start(bf16[2,3,48,256]{3,2,1,0:T(8,128)(2,1)S(1)} %get-tuple-element.320), channel_id=1, source_target_pairs={{0,8},{8,0},{16,24},{24,16},{1,9},{9,1},{17,25},{25,17},{2,10},{10... | collective-permute-start | bytes 442376 | tf_op jit(solution)/shard_map/ppermute | solution.py:64
  75.0 24.4 %collective-permute-start.13 = (bf16[4,3,48,256]{3,2,1,0:T(8,128)(2,1)S(1)}, bf16[4,3,48,256]{3,2,1,0:T(8,128)(2,1)S(1)}, u32[]{:S(2)}, u32[]{:S(2)}) collective-permute-start(bf16[4,3,48,256]{3,2,1,0:T(8,128)(2,1)S(1)} %get-tuple-element.308), channel_id=1, source_target_pairs={{0,2},{1,3},{2,0},{3,1},{4,6},{5,7},{6,4},{7,5},{8,10},{9,11},{10,... | collective-permute-start | bytes 884744 | tf_op jit(solution)/shard_map/ppermute | solution.py:64
  84.2 11.1 %collective-permute-start.25 = (bf16[2,3,48,256]{3,2,1,0:T(8,128)(2,1)S(1)}, bf16[2,3,48,256]{3,2,1,0:T(8,128)(2,1)S(1)}, u32[]{:S(2)}, u32[]{:S(2)}) collective-permute-start(bf16[2,3,48,256]{3,2,1,0:T(8,128)(2,1)S(1)} %get-tuple-element.333), channel_id=1, source_target_pairs={{0,8},{8,0},{16,24},{24,16},{1,9},{9,1},{17,25},{25,17},{2,10},{10... | collective-permute-start | bytes 442376 | tf_op jit(solution)/shard_map/ppermute | solution.py:64
  94.6 24.5 %collective-permute-start.40 = (bf16[4,3,48,256]{3,2,1,0:T(8,128)(2,1)S(1)}, bf16[4,3,48,256]{3,2,1,0:T(8,128)(2,1)S(1)}, u32[]{:S(2)}, u32[]{:S(2)}) collective-permute-start(bf16[4,3,48,256]{3,2,1,0:T(8,128)(2,1)S(1)} %stack_blocks.7.refs_0_), channel_id=1, source_target_pairs={{0,2},{1,3},{2,0},{3,1},{4,6},{5,7},{6,4},{7,5},{8,10},{9,11},{10,... | collective-permute-start | bytes 884744 | tf_op jit(solution)/shard_map/ppermute | solution.py:64
  95.3 14.8 %collective-permute-start.35 = (bf16[2,3,48,256]{3,2,1,0:T(8,128)(2,1)S(1)}, bf16[2,3,48,256]{3,2,1,0:T(8,128)(2,1)S(1)}, u32[]{:S(2)}, u32[]{:S(2)}) collective-permute-start(bf16[2,3,48,256]{3,2,1,0:T(8,128)(2,1)S(1)} %get-tuple-element.345), channel_id=1, source_target_pairs={{0,8},{8,0},{16,24},{24,16},{1,9},{9,1},{17,25},{25,17},{2,10},{10... | collective-permute-start | bytes 442376 | tf_op jit(solution)/shard_map/ppermute | solution.py:64
  102.8 11.7 %collective-permute-start.30 = (bf16[2,3,48,256]{3,2,1,0:T(8,128)(2,1)S(1)}, bf16[2,3,48,256]{3,2,1,0:T(8,128)(2,1)S(1)}, u32[]{:S(2)}, u32[]{:S(2)}) collective-permute-start(bf16[2,3,48,256]{3,2,1,0:T(8,128)(2,1)S(1)} %get-tuple-element.359), channel_id=1, source_target_pairs={{0,8},{8,0},{16,24},{24,16},{1,9},{9,1},{17,25},{25,17},{2,10},{10... | collective-permute-start | bytes 442376 | tf_op jit(solution)/shard_map/ppermute | solution.py:64
  114.0 15.5 %collective-permute-start.39 = (bf16[4,3,48,256]{3,2,1,0:T(8,128)(2,1)S(1)}, bf16[4,3,48,256]{3,2,1,0:T(8,128)(2,1)S(1)}, u32[]{:S(2)}, u32[]{:S(2)}) collective-permute-start(bf16[4,3,48,256]{3,2,1,0:T(8,128)(2,1)S(1)} %stack_blocks.7.refs_0_), channel_id=1, source_target_pairs={{0,1},{1,0},{2,3},{3,2},{4,5},{5,4},{6,7},{7,6},{8,9},{9,8},{10,11... | collective-permute-start | bytes 884744 | tf_op jit(solution)/shard_map/ppermute | solution.py:64
  119.1 13.6 %collective-permute-start.50 = (bf16[4,3,48,256]{3,2,1,0:T(8,128)(2,1)S(1)}, bf16[4,3,48,256]{3,2,1,0:T(8,128)(2,1)S(1)}, u32[]{:S(2)}, u32[]{:S(2)}) collective-permute-start(bf16[4,3,48,256]{3,2,1,0:T(8,128)(2,1)S(1)} %stack_blocks.8.refs_0_), channel_id=1, source_target_pairs={{0,2},{1,3},{2,0},{3,1},{4,6},{5,7},{6,4},{7,5},{8,10},{9,11},{10,... | collective-permute-start | bytes 884744 | tf_op jit(solution)/shard_map/ppermute | solution.py:64
  129.4 15.7 %collective-permute-start.49 = (bf16[4,3,48,256]{3,2,1,0:T(8,128)(2,1)S(1)}, bf16[4,3,48,256]{3,2,1,0:T(8,128)(2,1)S(1)}, u32[]{:S(2)}, u32[]{:S(2)}) collective-permute-start(bf16[4,3,48,256]{3,2,1,0:T(8,128)(2,1)S(1)} %stack_blocks.8.refs_0_), channel_id=1, source_target_pairs={{0,1},{1,0},{2,3},{3,2},{4,5},{5,4},{6,7},{7,6},{8,9},{9,8},{10,11... | collective-permute-start | bytes 884744 | tf_op jit(solution)/shard_map/ppermute | solution.py:64
  132.7 12.4 %collective-permute-start.51 = (bf16[4,3,48,256]{3,2,1,0:T(8,128)(2,1)S(1)}, bf16[4,3,48,256]{3,2,1,0:T(8,128)(2,1)S(1)}, u32[]{:S(2)}, u32[]{:S(2)}) collective-permute-start(bf16[4,3,48,256]{3,2,1,0:T(8,128)(2,1)S(1)} %collective-permute-done.50.refs_2_), channel_id=1, source_target_pairs={{0,1},{1,0},{2,3},{3,2},{4,5},{5,4},{6,7},{7,6},{8,9},{9,8},{10,11... | collective-permute-start | bytes 884744 | tf_op jit(solution)/shard_map/ppermute | solution.py:64
  132.8 14.6 %collective-permute-start.48 = (bf16[4,3,48,256]{3,2,1,0:T(8,128)(2,1)S(1)}, bf16[4,3,48,256]{3,2,1,0:T(8,128)(2,1)S(1)}, u32[]{:S(2)}, u32[]{:S(2)}) collective-permute-start(bf16[4,3,48,256]{3,2,1,0:T(8,128)(2,1)S(1)} %stack_blocks.9.refs_0_), channel_id=1, source_target_pairs={{0,2},{1,3},{2,0},{3,1},{4,6},{5,7},{6,4},{7,5},{8,10},{9,11},{10,... | collective-permute-start | bytes 884744 | tf_op jit(solution)/shard_map/ppermute | solution.py:64
  141.4 17.9 %collective-permute-start.57 = (bf16[4,3,48,256]{3,2,1,0:T(8,128)(2,1)S(1)}, bf16[4,3,48,256]{3,2,1,0:T(8,128)(2,1)S(1)}, u32[]{:S(2)}, u32[]{:S(2)}) collective-permute-start(bf16[4,3,48,256]{3,2,1,0:T(8,128)(2,1)S(1)} %stack_blocks.9.refs_0_), channel_id=1, source_target_pairs={{0,1},{1,0},{2,3},{3,2},{4,5},{5,4},{6,7},{7,6},{8,9},{9,8},{10,11... | collective-permute-start | bytes 884744 | tf_op jit(solution)/shard_map/ppermute | solution.py:64
  147.4 11.9 %collective-permute-start.58 = (bf16[4,3,48,256]{3,2,1,0:T(8,128)(2,1)S(1)}, bf16[4,3,48,256]{3,2,1,0:T(8,128)(2,1)S(1)}, u32[]{:S(2)}, u32[]{:S(2)}) collective-permute-start(bf16[4,3,48,256]{3,2,1,0:T(8,128)(2,1)S(1)} %collective-permute-done.48.refs_2_), channel_id=1, source_target_pairs={{0,1},{1,0},{2,3},{3,2},{4,5},{5,4},{6,7},{7,6},{8,9},{9,8},{10,11... | collective-permute-start | bytes 884744 | tf_op jit(solution)/shard_map/ppermute | solution.py:64
  147.5 14.2 %collective-permute-start.56 = (bf16[4,3,48,256]{3,2,1,0:T(8,128)(2,1)S(1)}, bf16[4,3,48,256]{3,2,1,0:T(8,128)(2,1)S(1)}, u32[]{:S(2)}, u32[]{:S(2)}) collective-permute-start(bf16[4,3,48,256]{3,2,1,0:T(8,128)(2,1)S(1)} %stack_blocks.10.refs_0_), channel_id=1, source_target_pairs={{0,2},{1,3},{2,0},{3,1},{4,6},{5,7},{6,4},{7,5},{8,10},{9,11},{10,... | collective-permute-start | bytes 884744 | tf_op jit(solution)/shard_map/ppermute | solution.py:64
  155.3 13.9 %collective-permute-start.67 = (bf16[4,3,48,256]{3,2,1,0:T(8,128)(2,1)S(1)}, bf16[4,3,48,256]{3,2,1,0:T(8,128)(2,1)S(1)}, u32[]{:S(2)}, u32[]{:S(2)}) collective-permute-start(bf16[4,3,48,256]{3,2,1,0:T(8,128)(2,1)S(1)} %stack_blocks.10.refs_0_), channel_id=1, source_target_pairs={{0,1},{1,0},{2,3},{3,2},{4,5},{5,4},{6,7},{7,6},{8,9},{9,8},{10,11... | collective-permute-start | bytes 884744 | tf_op jit(solution)/shard_map/ppermute | solution.py:64
  172.6 13.0 %collective-permute-start.63 = (bf16[4,3,48,256]{3,2,1,0:T(8,128)(2,1)S(1)}, bf16[4,3,48,256]{3,2,1,0:T(8,128)(2,1)S(1)}, u32[]{:S(2)}, u32[]{:S(2)}) collective-permute-start(bf16[4,3,48,256]{3,2,1,0:T(8,128)(2,1)S(1)} %stack_blocks.12.refs_0_), channel_id=1, source_target_pairs={{0,1},{1,0},{2,3},{3,2},{4,5},{5,4},{6,7},{7,6},{8,9},{9,8},{10,11... | collective-permute-start | bytes 884744 | tf_op jit(solution)/shard_map/ppermute | solution.py:64
  182.0 11.7 %collective-permute-start.61 = (bf16[4,3,48,256]{3,2,1,0:T(8,128)(2,1)S(1)}, bf16[4,3,48,256]{3,2,1,0:T(8,128)(2,1)S(1)}, u32[]{:S(2)}, u32[]{:S(2)}) collective-permute-start(bf16[4,3,48,256]{3,2,1,0:T(8,128)(2,1)S(1)} %stack_blocks.13.refs_0_), channel_id=1, source_target_pairs={{0,1},{1,0},{2,3},{3,2},{4,5},{5,4},{6,7},{7,6},{8,9},{9,8},{10,11... | collective-permute-start | bytes 884744 | tf_op jit(solution)/shard_map/ppermute | solution.py:64
  196.6 11.5 %collective-permute-start.72 = (f32[96,512]{1,0:T(8,128)S(1)}, f32[96,512]{1,0:T(8,128)S(1)}, u32[]{:S(2)}, u32[]{:S(2)}) collective-permute-start(f32[96,512]{1,0:T(8,128)S(1)} %get-tuple-element.466), channel_id=1, source_target_pairs={{0,4},{4,0},{1,5},{5,1},{2,6},{6,2},{3,7},{7,3},{8,12},{12,8},{9,1... | collective-permute-start | bytes 589832 | tf_op jit(solution)/shard_map/ppermute | solution.py:64
  (56 other events, 625.0 us)
